TPU v7x, 16 devices: a whole 2x2x2 slice. The times are simulated.
16 devices in a mesh: dp: 1, sp: 16 (over x, y, z, core).
Axes of the slice: x: 2, y: 2, z: 2, core: 2. Of those that a mesh axis runs over, the one named last changes fastest.
Arguments:
- q: bfloat16 [32, 8, 256], P('dp')
- k: bfloat16 [32, 8192, 8, 256], P('dp', 'sp')
- v: bfloat16 [32, 8192, 8, 256], P('dp', 'sp')
Outputs:
- q: bfloat16 [32, 8, 256], P('dp')
All inputs are finite; a program needn't handle non-finite values.
Results may differ from a plain program's by a relative error of at most 0.012.
Values are sent between devices in bfloat16 or wider.
A program may use at most 2 GiB of HBM per device.

v0:
```python
import jax
import jax.numpy as jnp
from jax import lax
from jax.sharding import PartitionSpec as P


def einsum(form, a, b):
    return jnp.einsum(form, a.astype(jnp.float32), b.astype(jnp.float32))


def part_of(q, k, v):
    grouped = q.reshape(q.shape[0], k.shape[2], -1, q.shape[2])
    scores = einsum("bgsd,bugd->bgsu", grouped, k) * q.shape[2] ** -0.5
    high = jnp.max(scores, -1, keepdims=True)
    weights = jnp.exp(scores - high)
    seen = einsum("bgsu,bugd->bgsd", weights.astype(jnp.bfloat16), v)
    return jnp.concatenate([seen, jnp.sum(weights, -1, keepdims=True), high], -1)


def together(parts):
    seen, total, high = parts[..., :-2], parts[..., -2:-1], parts[..., -1:]
    scale = jnp.exp(high - jnp.max(high, 0))
    return (jnp.sum(seen * scale, 0) / jnp.sum(total * scale, 0)).astype(jnp.bfloat16)


def solution(mesh):
    def step(q, k, v):
        return together(lax.all_gather(part_of(q, k, v), "sp")).reshape(q.shape)

    return jax.shard_map(
        step,
        mesh=mesh,
        in_specs=(P("dp", None, None), P("dp", "sp", None, None), P("dp", "sp", None, None)),
        out_specs=P("dp", None, None),
        check_vma=False,
    )
```

profile of v0, /device:TPU:0, one launch (start us, length us, event | category | flops | bytes accessed | tf_op | source)
XLA Modules:
  0.0 136.3 jit_solution(6681061146055471360)
XLA Ops:
  6.5 0.0 all-gather.3.cloned.1.call-start
  6.5 31.9 %fusion.2 = f32[32,8,1,512]{3,2,1,0:T(1,128)S(1)} fusion(bf16[32,512,8,256]{3,2,1,0:T(8,128)(2,1)} %param.4, bf16[32,8,256,1]{2,1,0,3:T(8,128)(2,1)} %bitcast.27), kind=kOutput, calls=%fused_computation.2 | convolution fusion | flops 67108864 | bytes 67764224 | tf_op jit(solution)/shard_map/bgsd,bugd->bgsu/dot_general | solution.py:8
  38.4 0.1 fusion.9
  38.5 0.2 fusion.10
  38.8 32.6 %fusion = f32[32,8,1,256]{3,2,1,0:T(1,128)S(1)} fusion(bf16[32,512,8,256]{3,2,1,0:T(8,128)(2,1)} %param.5, bf16[32,8,512,1]{2,1,0,3:T(8,128)(2,1)S(1)} %get-tuple-element.7), kind=kOutput, calls=%fused_computation | convolution fusion | flops 67108864 | bytes 67633152 | tf_op jit(solution)/shard_map/bgsu,bugd->bgsd/dot_general | solution.py:8
  71.4 0.3 copy.23
  71.7 0.3 copy.22
  72.0 0.9 pad_maximum_fusion
  72.8 0.0 all-gather.3.cloned.1.call-update
  72.9 44.8 %all-gather.3.cloned.1.call-done = f32[512,8,1,258]{3,1,2,0:T(8,128)} async-done(((f32[32,8,1,258]{3,1,2,0:T(8,128)}), f32[512,8,1,258]{3,1,2,0:T(8,128)}) %all-gather.3.cloned.1.call-update) | async-done | bytes 4227088 | tf_op jit(solution)/shard_map/all_gather | solution.py:28
  117.6 2.3 %slice_reduce_fusion = f32[32,8]{1,0:T(8,128)S(1)} fusion(f32[16,32,8,1,258]{4,2,1,0,3:T(8,128)} %bitcast.22), kind=kLoop, calls=%fused_computation.9 | loop fusion | flops 3840 | bytes 17408 | tf_op jit(solution)/shard_map/reduce_max | solution.py:22
  119.9 3.0 %fusion.5 = (f32[32,8]{1,0:T(8,128)S(1)}, f32[16,32,8,1,1]{4,2,1,0,3:T(8,128)S(1)}) fusion(f32[16,32,8,1,258]{4,2,1,0,3:T(8,128)} %bitcast.23, f32[32,8]{1,0:T(8,128)S(1)} %slice_reduce_fusion), kind=kLoop, calls=%fused_computation.7 | loop fusion | flops 12032 | bytes 51200 | tf_op jit(solution)/shard_map/reduce_sum | solution.py:23
  122.9 3.1 %copy.36 = f32[16,32,8,1,1]{2,1,0,3,4:T(8,128)S(1)} copy(f32[16,32,8,1,1]{4,2,1,0,3:T(8,128)S(1)} %get-tuple-element.6) | data formatting | bytes 32768 | tf_op jit(solution)/shard_map/mul | solution.py:23
  126.0 2.7 %fusion.4 = f32[32,8,256]{2,1,0:T(8,128)S(1)} fusion(f32[16,32,8,1,258]{4,2,1,0,3:T(8,128)} %bitcast.24, f32[16,32,8]{2,1,0:T(8,128)S(1)} %bitcast.25), kind=kLoop, calls=%fused_computation.5 | loop fusion | flops 2031616 | bytes 4472832 | tf_op jit(solution)/shard_map/reduce_sum | solution.py:23
  128.7 0.8 divide_convert_fusion
  (1 shorter events, 0.0 us)
Async XLA Ops:
  6.5 111.1 %all-gather.3.cloned.1.call-start = ((), (), s32[]{:S(2)}) async-start(), calls=%async_computation | async-start | bytes 6684672 | tf_op jit(solution)/shard_map/all_gather | solution.py:28
Sparse Core Ops, SparseCore 0:
  73.0 44.5 all-gather.2
where the time goes:
time: 136 us
  matrix products  64.5 us (47%)
  waiting for transfers between devices  44.8 us (33%)
  between operations  13.4 us (10%)
  other arithmetic  9.95 us (7%)
  local copies, waits for them, and re-layouts  3.6 us (3%)
    dot_general x2, matrix products, einsum(): return jnp.einsum(form, a.astype(jnp.float32), b.astype(jnp.float32))  64.5 us
    all_gather x1, waiting for transfers between devices, step(): return together(lax.all_gather(part_of(q, k, v), 'sp')).reshape(q.shape)  44.8 us
    mul x1, local copies, waits for them, and re-layouts, together(): seen * scale  3.06 us
    reduce_sum x1, other arithmetic, together(): jnp.sum(total * scale, 0)  3 us
  transfers between devices with their start and end apart: 1, of which 1 were waited for; matrix products, arithmetic and copies ran while one was open for 0% of the time, Pallas kernels for 0%

commit v1 on v0

v1 whole, which is shorter than its diff:
```python
import functools

import jax
import jax.numpy as jnp
from jax import lax
from jax.experimental import pallas as pl
from jax.experimental.pallas import tpu as pltpu
from jax.sharding import PartitionSpec as P

SLOTS = 5
LAG = 4
TAIL = 4
LOG2E = 1.4426950408889634


def tree(op, parts):
    while len(parts) > 1:
        parts = [op(*parts[i : i + 2]) if i + 1 < len(parts) else parts[i] for i in range(0, len(parts), 2)]
    return parts[0]


def attend(n, q_hbm, k_hbm, v_hbm, o_hbm, q_ref, kbuf, vbuf, scores, parts, stats, done, qsem, ksem, vsem, osem, psend, precv, ssend, srecv, dsend, drecv):
    batch, heads, head = q_ref.shape
    rows = k_hbm.shape[1]
    shared = batch - TAIL
    me = lax.axis_index("sp")

    def kcopy(b):
        slot = lax.rem(b, SLOTS)
        return pltpu.make_async_copy(k_hbm.at[b], kbuf.at[slot], ksem.at[slot])

    def vcopy(b):
        slot = lax.rem(b, SLOTS)
        return pltpu.make_async_copy(v_hbm.at[b], vbuf.at[slot], vsem.at[slot])

    def remote(ref, send, recv, peer):
        return pltpu.make_async_remote_copy(ref, ref, send, recv, device_id={"sp": peer}, device_id_type=pl.DeviceIdType.MESH)

    def part_to(b, peer):
        return (
            remote(parts.at[b, me], psend.at[b], precv.at[b], peer),
            remote(stats.at[b, me], ssend.at[b], srecv.at[b], peer),
        )

    def parts_of_others(b):
        some = pl.ds(0, n - 1)
        return (
            remote(parts.at[b, some], psend.at[b], precv.at[b], me),
            remote(stats.at[b, some], ssend.at[b], srecv.at[b], me),
        )

    def done_to(b, peer):
        return remote(done.at[b], dsend.at[b], drecv.at[b], peer)

    def done_to_others(b):
        some = pl.ds(0, n - 1)
        return remote(done.at[some], dsend.at[b], drecv.at[b], me)

    def others():
        return [lax.rem(me + j, n) for j in range(1, n)]

    lane = lax.broadcasted_iota(jnp.int32, (heads, 128), 1)
    sublane = lax.broadcasted_iota(jnp.int32, (heads, 128), 0)
    own = lax.rem(lane, heads) == sublane

    def turn(b, first=False, last=False):
        tiles = rows // 256
        if not first:
            high = tree(jnp.maximum, [jnp.where(own, scores[:, pl.ds(128 * i, 128)], -jnp.inf) for i in range(rows // 128)])
            high = jnp.max(high, -1, keepdims=True)
            weights = [jnp.exp2(jnp.where(own, (scores[:, pl.ds(128 * i, 128)] - high) * (head**-0.5 * LOG2E), -jnp.inf)) for i in range(rows // 128)]
            total = jnp.sum(tree(jnp.add, weights), -1, keepdims=True)
            weights = [w.astype(jnp.bfloat16) for w in weights]
        seen = None
        slot, vslot = lax.rem(b, SLOTS), lax.rem(b + SLOTS - 1, SLOTS)
        kept = []
        for t in range(tiles + LAG):
            if t < tiles and not last:
                kept.append(lax.dot_general(q_ref[b], kbuf[slot, pl.ds(256 * t, 256)], (((1,), (1,)), ((), ())), preferred_element_type=jnp.float32))
            if t >= LAG and not first:
                u = t - LAG
                w = jnp.concatenate([weights[2 * u], weights[2 * u + 1]], -1)
                d = jnp.dot(w, vbuf[vslot, pl.ds(256 * u, 256)], preferred_element_type=jnp.float32)
                seen = d if seen is None else seen + d
        for t, s in enumerate(kept):
            scores[:, pl.ds(256 * t, 256)] = s
        if not first:
            parts[b - 1, me] = seen.astype(jnp.bfloat16)
            row = jnp.where(lane == sublane, high * head**-0.5, 0.0) + jnp.where(lane == sublane + heads, total, 0.0)
            stats[b - 1, me] = jnp.sum(row, 0, keepdims=True)

    def combine(b):
        high, total = [], []
        for i in range(n):
            row = jnp.broadcast_to(stats[b, i], (heads, 128))
            high.append(jnp.sum(jnp.where(lane == sublane, row, 0.0), -1, keepdims=True))
            total.append(jnp.sum(jnp.where(lane == sublane + heads, row, 0.0), -1, keepdims=True))
        top = tree(jnp.maximum, high)
        scale = [jnp.exp(h - top) for h in high]
        total = tree(jnp.add, [t * s for t, s in zip(total, scale)])
        seen = tree(jnp.add, [parts[b, i].astype(jnp.float32) * s for i, s in enumerate(scale)])
        done[b] = (seen / total).astype(jnp.bfloat16)

    def send(b):
        owner = lax.rem(b, n)

        @pl.when(me != owner)
        def _():
            for copy in part_to(b, owner):
                copy.start()

    def own_up(b):
        owner = lax.rem(b, n)

        @pl.when(me == owner)
        def _():
            for copy in parts_of_others(b):
                copy.wait_recv()
            combine(b)
            for peer in others():
                done_to(b, peer).start()

        @pl.when(me != owner)
        def _():
            for copy in part_to(b, owner):
                copy.wait_send()

    def settle(b):
        owner = lax.rem(b, n)

        @pl.when(me == owner)
        def _():
            done_to_others(b).wait_send()

        @pl.when(me != owner)
        def _():
            done_to(b, owner).wait_recv()

    def send_all(b):
        for peer in others():
            for copy in part_to(b, peer):
                copy.start()

    def gather(b):
        for copy in parts_of_others(b):
            copy.wait_recv()
        combine(b)

    qcopy = pltpu.make_async_copy(q_hbm, q_ref, qsem)
    qcopy.start()
    for b in range(SLOTS):
        kcopy(b).start()
        vcopy(b).start()

    barrier = pltpu.get_barrier_semaphore()
    for peer in others():
        pl.semaphore_signal(barrier, 1, device_id={"sp": peer}, device_id_type=pl.DeviceIdType.MESH)
    pl.semaphore_wait(barrier, n - 1)

    qcopy.wait()
    kcopy(0).wait()
    turn(0, first=True)

    def body(b, _):
        @pl.when(b + SLOTS - 1 < batch)
        def _():
            kcopy(b + SLOTS - 1).start()

        @pl.when(b >= 2)
        def _():
            send(b - 2)

        @pl.when(b >= 4)
        def _():
            own_up(b - 4)

        @pl.when(b >= 8)
        def _():
            settle(b - 8)

        kcopy(b).wait()
        vcopy(b - 1).wait()
        turn(b)

        @pl.when(b + SLOTS - 1 < batch)
        def _():
            vcopy(b + SLOTS - 1).start()

    lax.fori_loop(1, shared + 1, body, None)
    for b in range(shared + 1, batch + 1):
        if b - 2 < shared:
            send(b - 2)
        else:
            send_all(b - 2)
        if b - 4 < shared:
            own_up(b - 4)
        if b - 8 < shared:
            settle(b - 8)
        if b < batch:
            kcopy(b).wait()
        vcopy(b - 1).wait()
        turn(b, last=b == batch)
    send_all(batch - 1)
    for b in range(batch - 3, shared):
        own_up(b)
    for b in range(shared, batch - 1):
        gather(b)
    for b in range(batch - 7, shared):
        settle(b)
    early = pltpu.make_async_copy(done.at[pl.ds(0, batch - 1)], o_hbm.at[pl.ds(0, batch - 1)], osem.at[0])
    early.start()
    gather(batch - 1)
    late = pltpu.make_async_copy(done.at[pl.ds(batch - 1, 1)], o_hbm.at[pl.ds(batch - 1, 1)], osem.at[1])
    late.start()
    for b in range(shared, batch):
        for copy in parts_of_others(b):
            copy.wait_send()
    early.wait()
    late.wait()


def solution(mesh):
    n = mesh.shape["sp"]

    def step(q, k, v):
        batch, tokens, heads, head = k.shape
        rows = tokens * heads
        return pl.pallas_call(
            functools.partial(attend, n),
            out_shape=jax.ShapeDtypeStruct(q.shape, q.dtype),
            in_specs=[pl.BlockSpec(memory_space=pl.ANY)] * 3,
            out_specs=pl.BlockSpec(memory_space=pl.ANY),
            scratch_shapes=[
                pltpu.VMEM((batch, heads, head), jnp.bfloat16),
                pltpu.VMEM((SLOTS, rows, head), jnp.bfloat16),
                pltpu.VMEM((SLOTS, rows, head), jnp.bfloat16),
                pltpu.VMEM((heads, rows), jnp.float32),
                pltpu.VMEM((batch, n, heads, head), jnp.bfloat16),
                pltpu.VMEM((batch, n, 1, 128), jnp.float32),
                pltpu.VMEM((batch, heads, head), jnp.bfloat16),
                pltpu.SemaphoreType.DMA,
                pltpu.SemaphoreType.DMA((SLOTS,)),
                pltpu.SemaphoreType.DMA((SLOTS,)),
                pltpu.SemaphoreType.DMA((2,)),
                *[pltpu.SemaphoreType.DMA((batch,))] * 6,
            ],
            compiler_params=pltpu.CompilerParams(vmem_limit_bytes=56 * 2**20, collective_id=0, has_side_effects=True),
        )(q, k.reshape(batch, rows, head), v.reshape(batch, rows, head))

    return jax.shard_map(
        step,
        mesh=mesh,
        in_specs=(P("dp", None, None), P("dp", "sp", None, None), P("dp", "sp", None, None)),
        out_specs=P("dp", None, None),
        check_vma=False,
    )
```

time: 136 us -> 56.9 us (0.42)
  matrix products: 64.5 us -> 0 us
  Pallas kernels: 0 us -> 55.2 us
  waiting for transfers between devices: 44.8 us -> 0 us
  between operations: 13.4 us -> 0.01 us
  other arithmetic: 9.95 us -> 0 us
  local copies, waits for them, and re-layouts: 3.6 us -> 1.57 us
    dot_general x2 -> x0, matrix products: 64.5 us -> none  [einsum(): return jnp.einsum(form, a.astype(jnp.float32), b.astype(jnp.float32))]
    pallas_call x0 -> x1, Pallas kernels: none -> 55.2 us  [step(): pl.pallas_call(functools.partial(attend, n), out_shape=jax.ShapeDtypeStru...]
    all_gather x1 -> x0, waiting for transfers between devices: 44.8 us -> none  [step(): return together(lax.all_gather(part_of(q, k, v), 'sp')).reshape(q.shape)]
    reduce_sum x2 -> x0, other arithmetic: 5.68 us -> none  [the longest x1 3 us: together(): jnp.sum(total * scale, 0)]
    mul x1 -> x0, local copies, waits for them, and re-layouts: 3.06 us -> none  [together(): seen * scale]
    reduce_max x2 -> x0, other arithmetic: 2.4 us -> none  [the longest x1 2.27 us: together(): scale = jnp.exp(high - jnp.max(high, 0))]
    unnamed x0 -> x1, local copies, waits for them, and re-layouts: none -> 1.57 us
  transfers between devices with their start and end apart: 1 -> 0, of which waited for: 1 -> 0; matrix products, arithmetic and copies ran while one was open for 0% -> 0% of each run, Pallas kernels for 0% -> 0%
where the time goes in v1:
time: 56.9 us; the launch traced here: 56.8 us
  Pallas kernels  55.2 us (97%)
  local copies, waits for them, and re-layouts  1.57 us (3%)
    pallas_call x1, Pallas kernels, step(): pl.pallas_call(functools.partial(attend, n), out_shape=jax.ShapeDtypeStru...  55.2 us
    unnamed x1, local copies, waits for them, and re-layouts  1.57 us

profile of v1, /device:TPU:0, one launch (start us, length us, event | category | flops | bytes accessed | tf_op | source)
XLA Modules:
  0.0 56.8 jit_solution(14650859247444198010)
XLA Ops:
  0.0 55.2 %shard_map.37 = bf16[32,8,256]{2,1,0:T(8,128)(2,1)} custom-call(bf16[32,8,256]{2,1,0:T(8,128)(2,1)} %q_hbm.1, bf16[32,4096,256]{2,1,0:T(8,128)(2,1)} %bitcast.k_hbm, bf16[32,4096,256]{2,1,0:T(8,128)(2,1)} %bitcast.1.v_hbm), custom_call_target="tpu_custom_call" | custom-call | tf_op jit(solution)/shard_map/pallas_call | solution.py:228
  55.2 1.6 %copy.5 = bf16[32,8,256]{2,1,0:T(8,128)(2,1)} copy(bf16[32,8,256]{2,1,0:T(8,128)(2,1)} %shard_map.37) | data formatting | bytes 262144

commit v2 on v1

v2 whole, which is shorter than its diff:
```python
import functools

import jax
import jax.numpy as jnp
from jax import lax
from jax.experimental import pallas as pl
from jax.experimental.pallas import tpu as pltpu
from jax.sharding import PartitionSpec as P

SLOTS = 5
LAG = 4
WAIT = 6
TAIL = 6
LOG2E = 1.4426950408889634


def tree(op, parts):
    while len(parts) > 1:
        parts = [op(*parts[i : i + 2]) if i + 1 < len(parts) else parts[i] for i in range(0, len(parts), 2)]
    return parts[0]


def attend(n, q_hbm, k_hbm, v_hbm, done, q_ref, kbuf, vbuf, scores, parts, stats, qsem, ksem, vsem, psend, ssend, dsend, drecv, precv, srecv):
    batch, heads, head = q_ref.shape
    rows = k_hbm.shape[1]
    shared = batch - TAIL
    me = lax.axis_index("sp")

    def kcopy(b):
        slot = lax.rem(b, SLOTS)
        return pltpu.make_async_copy(k_hbm.at[b], kbuf.at[slot], ksem.at[slot])

    def vcopy(b):
        slot = lax.rem(b, SLOTS)
        return pltpu.make_async_copy(v_hbm.at[b], vbuf.at[slot], vsem.at[slot])

    def remote(ref, send, recv, peer):
        return pltpu.make_async_remote_copy(ref, ref, send, recv, device_id={"sp": peer}, device_id_type=pl.DeviceIdType.MESH)

    def others():
        return [lax.rem(me + j, n) for j in range(1, n)]

    def send_part(b, sem, peer):
        remote(parts.at[b, me], psend, precv.at[sem], peer).start()
        remote(stats.at[b, me], ssend, srecv.at[sem], peer).start()

    lane = lax.broadcasted_iota(jnp.int32, (heads, 128), 1)
    sublane = lax.broadcasted_iota(jnp.int32, (heads, 128), 0)
    own = lax.rem(lane, heads) == sublane

    def turn(b, first=False, last=False):
        tiles = rows // 256
        if not first:
            high = tree(jnp.maximum, [jnp.where(own, scores[:, pl.ds(128 * i, 128)], -jnp.inf) for i in range(rows // 128)])
            high = jnp.max(high, -1, keepdims=True)
            weights = [jnp.exp2(jnp.where(own, (scores[:, pl.ds(128 * i, 128)] - high) * (head**-0.5 * LOG2E), -jnp.inf)) for i in range(rows // 128)]
            total = jnp.sum(tree(jnp.add, weights), -1, keepdims=True)
            weights = [w.astype(jnp.bfloat16) for w in weights]
        seen = None
        slot, vslot = lax.rem(b, SLOTS), lax.rem(b + SLOTS - 1, SLOTS)
        kept = []
        for t in range(tiles + LAG):
            if t < tiles and not last:
                kept.append(lax.dot_general(q_ref[b], kbuf[slot, pl.ds(256 * t, 256)], (((1,), (1,)), ((), ())), preferred_element_type=jnp.float32))
            if t >= LAG and not first:
                u = t - LAG
                w = jnp.concatenate([weights[2 * u], weights[2 * u + 1]], -1)
                d = jnp.dot(w, vbuf[vslot, pl.ds(256 * u, 256)], preferred_element_type=jnp.float32)
                seen = d if seen is None else seen + d
        for t, s in enumerate(kept):
            scores[:, pl.ds(256 * t, 256)] = s
        if not first:
            parts[b - 1, me] = seen.astype(jnp.bfloat16)
            row = jnp.where(lane == sublane, high * head**-0.5, 0.0) + jnp.where(lane == sublane + heads, total, 0.0)
            stats[b - 1, me] = jnp.sum(row, 0, keepdims=True)

    def gather(b, sem):
        some = pl.ds(0, n - 1)
        remote(parts.at[b, some], psend, precv.at[sem], me).wait_recv()
        remote(stats.at[b, some], ssend, srecv.at[sem], me).wait_recv()
        high, total = [], []
        for i in range(n):
            row = jnp.broadcast_to(stats[b, i], (heads, 128))
            high.append(jnp.sum(jnp.where(lane == sublane, row, 0.0), -1, keepdims=True))
            total.append(jnp.sum(jnp.where(lane == sublane + heads, row, 0.0), -1, keepdims=True))
        top = tree(jnp.maximum, high)
        scale = [jnp.exp(h - top) for h in high]
        total = tree(jnp.add, [t * s for t, s in zip(total, scale)])
        seen = tree(jnp.add, [parts[b, i].astype(jnp.float32) * s for i, s in enumerate(scale)])
        done[b] = (seen / total).astype(jnp.bfloat16)

    def send(b):
        owner = lax.rem(b, n)

        @pl.when(me != owner)
        def _():
            send_part(b, b // n, owner)

    def own_up(b):
        @pl.when(me == lax.rem(b, n))
        def _():
            gather(b, b // n)
            for peer in others():
                remote(done.at[b], dsend, drecv, peer).start()

    def send_all(b):
        for peer in others():
            send_part(b, b - shared + pl.cdiv(shared, n), peer)

    qcopy = pltpu.make_async_copy(q_hbm, q_ref, qsem)
    qcopy.start()
    for b in range(SLOTS):
        kcopy(b).start()
        vcopy(b).start()

    barrier = pltpu.get_barrier_semaphore()
    for peer in others():
        pl.semaphore_signal(barrier, 1, device_id={"sp": peer}, device_id_type=pl.DeviceIdType.MESH)
    pl.semaphore_wait(barrier, n - 1)

    qcopy.wait()
    kcopy(0).wait()
    turn(0, first=True)

    def body(b, _):
        @pl.when(b + SLOTS - 1 < batch)
        def _():
            kcopy(b + SLOTS - 1).start()

        @pl.when((b >= 2) & (b - 2 < shared))
        def _():
            send(b - 2)

        @pl.when(b - 2 >= shared)
        def _():
            send_all(b - 2)

        @pl.when((b >= WAIT) & (b - WAIT < shared))
        def _():
            own_up(b - WAIT)

        kcopy(b).wait()
        vcopy(b - 1).wait()
        turn(b)

        @pl.when(b + SLOTS - 1 < batch)
        def _():
            vcopy(b + SLOTS - 1).start()

    lax.fori_loop(1, batch, body, None)
    send_all(batch - 2)
    vcopy(batch - 1).wait()
    turn(batch, last=True)
    send_all(batch - 1)
    for b in range(batch - WAIT, shared):
        own_up(b)
    for b in range(shared, batch):
        gather(b, b - shared + pl.cdiv(shared, n))

    for mine in {shared // n, pl.cdiv(shared, n)}:
        sent = shared - mine

        @pl.when((me < shared % n) == (mine > shared // n))
        def _():
            remote(done.at[pl.ds(0, sent)], dsend, drecv, me).wait_recv()
            for _ in range(mine):
                remote(done.at[pl.ds(0, n - 1)], dsend, drecv, me).wait_send()
            remote(parts.at[pl.ds(0, sent), 0], psend, precv.at[0], me).wait_send()
            remote(stats.at[pl.ds(0, sent), 0], ssend, srecv.at[0], me).wait_send()

    remote(parts.at[pl.ds(0, TAIL), pl.ds(0, n - 1)], psend, precv.at[0], me).wait_send()
    remote(stats.at[pl.ds(0, TAIL), pl.ds(0, n - 1)], ssend, srecv.at[0], me).wait_send()


def solution(mesh):
    n = mesh.shape["sp"]

    def step(q, k, v):
        batch, tokens, heads, head = k.shape
        rows = tokens * heads
        return pl.pallas_call(
            functools.partial(attend, n),
            out_shape=jax.ShapeDtypeStruct(q.shape, q.dtype),
            in_specs=[pl.BlockSpec(memory_space=pl.ANY)] * 3,
            out_specs=pl.BlockSpec(memory_space=pltpu.VMEM),
            scratch_shapes=[
                pltpu.VMEM((batch, heads, head), jnp.bfloat16),
                pltpu.VMEM((SLOTS, rows, head), jnp.bfloat16),
                pltpu.VMEM((SLOTS, rows, head), jnp.bfloat16),
                pltpu.VMEM((heads, rows), jnp.float32),
                pltpu.VMEM((batch, n, heads, head), jnp.bfloat16),
                pltpu.VMEM((batch, n, 1, 128), jnp.float32),
                pltpu.SemaphoreType.DMA,
                pltpu.SemaphoreType.DMA((SLOTS,)),
                pltpu.SemaphoreType.DMA((SLOTS,)),
                *[pltpu.SemaphoreType.DMA] * 4,
                *[pltpu.SemaphoreType.DMA((pl.cdiv(batch - TAIL, n) + TAIL,))] * 2,
            ],
            compiler_params=pltpu.CompilerParams(vmem_limit_bytes=215 * 2**18, collective_id=0, has_side_effects=True),
        )(q, k.reshape(batch, rows, head), v.reshape(batch, rows, head))

    return jax.shard_map(
        step,
        mesh=mesh,
        in_specs=(P("dp", None, None), P("dp", "sp", None, None), P("dp", "sp", None, None)),
        out_specs=P("dp", None, None),
        check_vma=False,
    )
```

time: 56.9 us -> 49.2 us (0.86)
  Pallas kernels: 55.2 us -> 48.4 us
  local copies, waits for them, and re-layouts: 1.57 us -> 0.66 us
    pallas_call x1, Pallas kernels: 55.2 us -> 48.4 us  [step(): pl.pallas_call(functools.partial(attend, n), out_shape=jax.ShapeDtypeStru...]
    unnamed x1, local copies, waits for them, and re-layouts: 1.57 us -> 0.66 us
where the time goes in v2:
time: 49.2 us; the launch traced here: 49.1 us
  Pallas kernels  48.4 us (98%)
  local copies, waits for them, and re-layouts  0.66 us (1%)
    pallas_call x1, Pallas kernels, step(): pl.pallas_call(functools.partial(attend, n), out_shape=jax.ShapeDtypeStru...  48.4 us

profile of v2, /device:TPU:0, one launch (start us, length us, event | category | flops | bytes accessed | tf_op | source)
XLA Modules:
  0.0 49.1 jit_solution(3035940842794587502)
XLA Ops:
  0.0 48.4 %shard_map.37 = bf16[32,8,256]{2,1,0:T(8,128)(2,1)S(1)} custom-call(bf16[32,8,256]{2,1,0:T(8,128)(2,1)} %q_hbm.1, bf16[32,4096,256]{2,1,0:T(8,128)(2,1)} %bitcast.k_hbm, bf16[32,4096,256]{2,1,0:T(8,128)(2,1)} %bitcast.1.v_hbm), custom_call_target="tpu_custom_call" | custom-call | tf_op jit(solution)/shard_map/pallas_call | solution.py:181
  48.4 0.7 %copy.5 = bf16[32,8,256]{2,1,0:T(8,128)(2,1)} copy(bf16[32,8,256]{2,1,0:T(8,128)(2,1)S(1)} %shard_map.37) | data formatting | bytes 262144

commit v3 on v2

--- a/solution.py
+++ b/solution.py
@@ -10,7 +10,7 @@
 SLOTS = 5
 LAG = 4
 WAIT = 6
-TAIL = 6
+TAIL = 8
 LOG2E = 1.4426950408889634
 
 
@@ -37,8 +37,7 @@
     def remote(ref, send, recv, peer):
         return pltpu.make_async_remote_copy(ref, ref, send, recv, device_id={"sp": peer}, device_id_type=pl.DeviceIdType.MESH)
 
-    def others():
-        return [lax.rem(me + j, n) for j in range(1, n)]
+    peers = [j + lax.div(n + j - me, n) for j in range(n - 1)]
 
     def send_part(b, sem, peer):
         remote(parts.at[b, me], psend, precv.at[sem], peer).start()
@@ -48,31 +47,41 @@
     sublane = lax.broadcasted_iota(jnp.int32, (heads, 128), 0)
     own = lax.rem(lane, heads) == sublane
 
-    def turn(b, first=False, last=False):
-        tiles = rows // 256
-        if not first:
-            high = tree(jnp.maximum, [jnp.where(own, scores[:, pl.ds(128 * i, 128)], -jnp.inf) for i in range(rows // 128)])
-            high = jnp.max(high, -1, keepdims=True)
-            weights = [jnp.exp2(jnp.where(own, (scores[:, pl.ds(128 * i, 128)] - high) * (head**-0.5 * LOG2E), -jnp.inf)) for i in range(rows // 128)]
-            total = jnp.sum(tree(jnp.add, weights), -1, keepdims=True)
-            weights = [w.astype(jnp.bfloat16) for w in weights]
-        seen = None
-        slot, vslot = lax.rem(b, SLOTS), lax.rem(b + SLOTS - 1, SLOTS)
-        kept = []
+    tiles = rows // 256
+
+    def scale_rows():
+        high = tree(jnp.maximum, [jnp.where(own, scores[:, pl.ds(128 * i, 128)], -jnp.inf) for i in range(rows // 128)])
+        high = jnp.max(high, -1, keepdims=True)
+        weights = [jnp.exp2(jnp.where(own, (scores[:, pl.ds(128 * i, 128)] - high) * (head**-0.5 * LOG2E), -jnp.inf)) for i in range(rows // 128)]
+        total = jnp.sum(tree(jnp.add, weights), -1, keepdims=True)
+        weights = [jnp.concatenate([w.astype(jnp.bfloat16) for w in weights[i : i + 2]], -1) for i in range(0, len(weights), 2)]
+        return weights, total, high
+
+    def score(b, t):
+        return lax.dot_general(q_ref[b], kbuf[lax.rem(b, SLOTS), pl.ds(256 * t, 256)], (((1,), (1,)), ((), ())), preferred_element_type=jnp.float32)
+
+    def value(b, t, weights):
+        return jnp.dot(weights[t], vbuf[lax.rem(b, SLOTS), pl.ds(256 * t, 256)], preferred_element_type=jnp.float32)
+
+    def keep(found):
+        for t, s in enumerate(found):
+            scores[:, pl.ds(256 * t, 256)] = s
+
+    def part(b, seen, total, high):
+        parts[b, me] = seen.astype(jnp.bfloat16)
+        row = jnp.where(lane == sublane, high * head**-0.5, 0.0) + jnp.where(lane == sublane + heads, total, 0.0)
+        stats[b, me] = jnp.sum(row, 0, keepdims=True)
+
+    def turn(b):
+        weights, total, high = scale_rows()
+        found, seen = [], []
         for t in range(tiles + LAG):
-            if t < tiles and not last:
-                kept.append(lax.dot_general(q_ref[b], kbuf[slot, pl.ds(256 * t, 256)], (((1,), (1,)), ((), ())), preferred_element_type=jnp.float32))
-            if t >= LAG and not first:
-                u = t - LAG
-                w = jnp.concatenate([weights[2 * u], weights[2 * u + 1]], -1)
-                d = jnp.dot(w, vbuf[vslot, pl.ds(256 * u, 256)], preferred_element_type=jnp.float32)
-                seen = d if seen is None else seen + d
-        for t, s in enumerate(kept):
-            scores[:, pl.ds(256 * t, 256)] = s
-        if not first:
-            parts[b - 1, me] = seen.astype(jnp.bfloat16)
-            row = jnp.where(lane == sublane, high * head**-0.5, 0.0) + jnp.where(lane == sublane + heads, total, 0.0)
-            stats[b - 1, me] = jnp.sum(row, 0, keepdims=True)
+            if t < tiles:
+                found.append(score(b, t))
+            if t >= LAG:
+                seen.append(value(b - 1, t - LAG, weights))
+        keep(found)
+        part(b - 1, functools.reduce(jnp.add, seen), total, high)
 
     def gather(b, sem):
         some = pl.ds(0, n - 1)
@@ -100,33 +109,32 @@
         @pl.when(me == lax.rem(b, n))
         def _():
             gather(b, b // n)
-            for peer in others():
+            for peer in peers:
                 remote(done.at[b], dsend, drecv, peer).start()
 
-    def send_all(b):
-        for peer in others():
+    def send_all(b, some=slice(None)):
+        for peer in peers[some]:
             send_part(b, b - shared + pl.cdiv(shared, n), peer)
 
     qcopy = pltpu.make_async_copy(q_hbm, q_ref, qsem)
     qcopy.start()
-    for b in range(SLOTS):
+    kcopy(0).start()
+    for b in range(1, SLOTS):
         kcopy(b).start()
-        vcopy(b).start()
+        vcopy(b - 1).start()
 
     barrier = pltpu.get_barrier_semaphore()
-    for peer in others():
+    for peer in peers:
         pl.semaphore_signal(barrier, 1, device_id={"sp": peer}, device_id_type=pl.DeviceIdType.MESH)
     pl.semaphore_wait(barrier, n - 1)
 
     qcopy.wait()
     kcopy(0).wait()
-    turn(0, first=True)
+    keep([score(0, t) for t in range(tiles)])
+    kcopy(SLOTS).start()
+    vcopy(SLOTS - 1).start()
 
     def body(b, _):
-        @pl.when(b + SLOTS - 1 < batch)
-        def _():
-            kcopy(b + SLOTS - 1).start()
-
         @pl.when((b >= 2) & (b - 2 < shared))
         def _():
             send(b - 2)
@@ -143,19 +151,30 @@
         vcopy(b - 1).wait()
         turn(b)
 
+        @pl.when(b + SLOTS < batch)
+        def _():
+            kcopy(b + SLOTS).start()
+
         @pl.when(b + SLOTS - 1 < batch)
         def _():
             vcopy(b + SLOTS - 1).start()
 
     lax.fori_loop(1, batch, body, None)
-    send_all(batch - 2)
+    weights, total, high = scale_rows()
+    send_all(batch - 2, slice(2))
     vcopy(batch - 1).wait()
-    turn(batch, last=True)
+    seen = [value(batch - 1, t, weights) for t in range(tiles)]
+    one, other = functools.reduce(jnp.add, seen[::2]), functools.reduce(jnp.add, seen[1::2])
+    part(batch - 1, one + jnp.where(me >= 0, other, 0.0), total, high)
     send_all(batch - 1)
+    send_all(batch - 2, slice(2, None))
     for b in range(batch - WAIT, shared):
         own_up(b)
-    for b in range(shared, batch):
+
+    def last(b, _):
         gather(b, b - shared + pl.cdiv(shared, n))
+
+    lax.fori_loop(shared, batch, last, None)
 
     for mine in {shared // n, pl.cdiv(shared, n)}:
         sent = shared - mine

time: 49.2 us -> 48.7 us (0.990)
  Pallas kernels: 48.4 us -> 47.9 us
where the time goes in v3:
time: 48.7 us; the launch traced here: 48.6 us
  Pallas kernels  47.9 us (98%)
  local copies, waits for them, and re-layouts  0.66 us (1%)
    pallas_call x1, Pallas kernels, step(): pl.pallas_call(functools.partial(attend, n), out_shape=jax.ShapeDtypeStru...  47.9 us

profile of v3, /device:TPU:0, one launch (start us, length us, event | category | flops | bytes accessed | tf_op | source)
XLA Modules:
  0.0 48.6 jit_solution(3421676804676269775)
XLA Ops:
  0.0 47.9 %shard_map.37 = bf16[32,8,256]{2,1,0:T(8,128)(2,1)S(1)} custom-call(bf16[32,8,256]{2,1,0:T(8,128)(2,1)} %q_hbm.1, bf16[32,4096,256]{2,1,0:T(8,128)(2,1)} %bitcast.k_hbm, bf16[32,4096,256]{2,1,0:T(8,128)(2,1)} %bitcast.1.v_hbm), custom_call_target="tpu_custom_call" | custom-call | tf_op jit(solution)/shard_map/pallas_call | solution.py:200
  47.9 0.7 %copy.5 = bf16[32,8,256]{2,1,0:T(8,128)(2,1)} copy(bf16[32,8,256]{2,1,0:T(8,128)(2,1)S(1)} %shard_map.37) | data formatting | bytes 262144

commit v4 on v3

--- a/solution.py
+++ b/solution.py
@@ -8,9 +8,10 @@
 from jax.sharding import PartitionSpec as P
 
 SLOTS = 5
+LEAD = 2
 LAG = 4
-WAIT = 6
-TAIL = 8
+WAIT = 7
+TAIL = 6
 LOG2E = 1.4426950408889634
 
 
@@ -49,10 +50,11 @@
 
     tiles = rows // 256
 
-    def scale_rows():
-        high = tree(jnp.maximum, [jnp.where(own, scores[:, pl.ds(128 * i, 128)], -jnp.inf) for i in range(rows // 128)])
+    def scale_rows(b):
+        row = scores.at[lax.rem(b, LEAD + 1)]
+        high = tree(jnp.maximum, [jnp.where(own, row[:, pl.ds(128 * i, 128)], -jnp.inf) for i in range(rows // 128)])
         high = jnp.max(high, -1, keepdims=True)
-        weights = [jnp.exp2(jnp.where(own, (scores[:, pl.ds(128 * i, 128)] - high) * (head**-0.5 * LOG2E), -jnp.inf)) for i in range(rows // 128)]
+        weights = [jnp.exp2(jnp.where(own, (row[:, pl.ds(128 * i, 128)] - high) * (head**-0.5 * LOG2E), -jnp.inf)) for i in range(rows // 128)]
         total = jnp.sum(tree(jnp.add, weights), -1, keepdims=True)
         weights = [jnp.concatenate([w.astype(jnp.bfloat16) for w in weights[i : i + 2]], -1) for i in range(0, len(weights), 2)]
         return weights, total, high
@@ -63,9 +65,9 @@
     def value(b, t, weights):
         return jnp.dot(weights[t], vbuf[lax.rem(b, SLOTS), pl.ds(256 * t, 256)], preferred_element_type=jnp.float32)
 
-    def keep(found):
+    def keep(b, found):
         for t, s in enumerate(found):
-            scores[:, pl.ds(256 * t, 256)] = s
+            scores[lax.rem(b, LEAD + 1), :, pl.ds(256 * t, 256)] = s
 
     def part(b, seen, total, high):
         parts[b, me] = seen.astype(jnp.bfloat16)
@@ -73,15 +75,20 @@
         stats[b, me] = jnp.sum(row, 0, keepdims=True)
 
     def turn(b):
-        weights, total, high = scale_rows()
+        weights, total, high = scale_rows(b - LEAD)
         found, seen = [], []
         for t in range(tiles + LAG):
             if t < tiles:
                 found.append(score(b, t))
             if t >= LAG:
-                seen.append(value(b - 1, t - LAG, weights))
-        keep(found)
-        part(b - 1, functools.reduce(jnp.add, seen), total, high)
+                seen.append(value(b - LEAD, t - LAG, weights))
+        keep(b, found)
+        part(b - LEAD, functools.reduce(jnp.add, seen), total, high)
+
+    def values(b, weights):
+        seen = [value(b, t, weights) for t in range(tiles)]
+        one, other = functools.reduce(jnp.add, seen[::2]), functools.reduce(jnp.add, seen[1::2])
+        return one + jnp.where(me >= 0, other, 0.0)
 
     def gather(b, sem):
         some = pl.ds(0, n - 1)
@@ -118,10 +125,10 @@
 
     qcopy = pltpu.make_async_copy(q_hbm, q_ref, qsem)
     qcopy.start()
-    kcopy(0).start()
-    for b in range(1, SLOTS):
+    for b in range(SLOTS):
         kcopy(b).start()
-        vcopy(b - 1).start()
+        if b >= LEAD:
+            vcopy(b - LEAD).start()
 
     barrier = pltpu.get_barrier_semaphore()
     for peer in peers:
@@ -129,45 +136,49 @@
     pl.semaphore_wait(barrier, n - 1)
 
     qcopy.wait()
-    kcopy(0).wait()
-    keep([score(0, t) for t in range(tiles)])
-    kcopy(SLOTS).start()
-    vcopy(SLOTS - 1).start()
+    for b in range(LEAD):
+        kcopy(b).wait()
+        keep(b, [score(b, t) for t in range(tiles)])
+        kcopy(b + SLOTS).start()
+        vcopy(b + SLOTS - LEAD).start()
 
     def body(b, _):
-        @pl.when((b >= 2) & (b - 2 < shared))
-        def _():
-            send(b - 2)
-
-        @pl.when(b - 2 >= shared)
-        def _():
-            send_all(b - 2)
+        @pl.when((b > LEAD) & (b - LEAD - 1 < shared))
+        def _():
+            send(b - LEAD - 1)
+
+        @pl.when(b - LEAD - 1 >= shared)
+        def _():
+            send_all(b - LEAD - 1)
 
         @pl.when((b >= WAIT) & (b - WAIT < shared))
         def _():
             own_up(b - WAIT)
 
         kcopy(b).wait()
-        vcopy(b - 1).wait()
+        vcopy(b - LEAD).wait()
         turn(b)
 
         @pl.when(b + SLOTS < batch)
         def _():
             kcopy(b + SLOTS).start()
 
-        @pl.when(b + SLOTS - 1 < batch)
-        def _():
-            vcopy(b + SLOTS - 1).start()
-
-    lax.fori_loop(1, batch, body, None)
-    weights, total, high = scale_rows()
-    send_all(batch - 2, slice(2))
-    vcopy(batch - 1).wait()
-    seen = [value(batch - 1, t, weights) for t in range(tiles)]
-    one, other = functools.reduce(jnp.add, seen[::2]), functools.reduce(jnp.add, seen[1::2])
-    part(batch - 1, one + jnp.where(me >= 0, other, 0.0), total, high)
+        @pl.when(b + SLOTS - LEAD < batch)
+        def _():
+            vcopy(b + SLOTS - LEAD).start()
+
+    lax.fori_loop(LEAD, batch, body, None)
+    ready = scale_rows(batch - LEAD)
+    for b in range(batch - LEAD, batch):
+        send_all(b - 1, slice(2))
+        vcopy(b).wait()
+        weights, total, high = ready
+        if b + 1 < batch:
+            ready = scale_rows(b + 1)
+        part(b, values(b, weights), total, high)
     send_all(batch - 1)
-    send_all(batch - 2, slice(2, None))
+    for b in range(batch - 2, batch - LEAD - 2, -1):
+        send_all(b, slice(2, None))
     for b in range(batch - WAIT, shared):
         own_up(b)
 
@@ -206,7 +217,7 @@
                 pltpu.VMEM((batch, heads, head), jnp.bfloat16),
                 pltpu.VMEM((SLOTS, rows, head), jnp.bfloat16),
                 pltpu.VMEM((SLOTS, rows, head), jnp.bfloat16),
-                pltpu.VMEM((heads, rows), jnp.float32),
+                pltpu.VMEM((LEAD + 1, heads, rows), jnp.float32),
                 pltpu.VMEM((batch, n, heads, head), jnp.bfloat16),
                 pltpu.VMEM((batch, n, 1, 128), jnp.float32),
                 pltpu.SemaphoreType.DMA,

time: 48.7 us -> 48.6 us (level)
  no operation moved by 1% of the time
where the time goes in v4:
time: 48.6 us; the launch traced here: 48.4 us
  Pallas kernels  47.8 us (98%)
  local copies, waits for them, and re-layouts  0.66 us (1%)
    pallas_call x1, Pallas kernels, step(): pl.pallas_call(functools.partial(attend, n), out_shape=jax.ShapeDtypeStru...  47.8 us

profile of v4, /device:TPU:0, one launch (start us, length us, event | category | flops | bytes accessed | tf_op | source)
XLA Modules:
  0.0 48.4 jit_solution(4303240099020817758)
XLA Ops:
  0.0 47.8 %shard_map.37 = bf16[32,8,256]{2,1,0:T(8,128)(2,1)S(1)} custom-call(bf16[32,8,256]{2,1,0:T(8,128)(2,1)} %q_hbm.1, bf16[32,4096,256]{2,1,0:T(8,128)(2,1)} %bitcast.k_hbm, bf16[32,4096,256]{2,1,0:T(8,128)(2,1)} %bitcast.1.v_hbm), custom_call_target="tpu_custom_call" | custom-call | tf_op jit(solution)/shard_map/pallas_call | solution.py:211
  47.8 0.7 %copy.5 = bf16[32,8,256]{2,1,0:T(8,128)(2,1)} copy(bf16[32,8,256]{2,1,0:T(8,128)(2,1)S(1)} %shard_map.37) | data formatting | bytes 262144

commit v5 on v4

--- a/solution.py
+++ b/solution.py
@@ -7,7 +7,7 @@
 from jax.experimental.pallas import tpu as pltpu
 from jax.sharding import PartitionSpec as P
 
-SLOTS = 5
+SLOTS = 4
 LEAD = 2
 LAG = 4
 WAIT = 7

time: 48.6 us -> 48.5 us (level)
  no operation moved by 1% of the time
where the time goes in v5:
time: 48.5 us; the launch traced here: 48.4 us
  Pallas kernels  47.8 us (99%)
  local copies, waits for them, and re-layouts  0.66 us (1%)
    pallas_call x1, Pallas kernels, step(): pl.pallas_call(functools.partial(attend, n), out_shape=jax.ShapeDtypeStru...  47.8 us

profile of v5, /device:TPU:0, one launch (start us, length us, event | category | flops | bytes accessed | tf_op | source)
XLA Modules:
  0.0 48.4 jit_solution(2289278070434586837)
XLA Ops:
  0.0 47.8 %shard_map.37 = bf16[32,8,256]{2,1,0:T(8,128)(2,1)S(1)} custom-call(bf16[32,8,256]{2,1,0:T(8,128)(2,1)} %q_hbm.1, bf16[32,4096,256]{2,1,0:T(8,128)(2,1)} %bitcast.k_hbm, bf16[32,4096,256]{2,1,0:T(8,128)(2,1)} %bitcast.1.v_hbm), custom_call_target="tpu_custom_call" | custom-call | tf_op jit(solution)/shard_map/pallas_call | solution.py:211
  47.8 0.7 %copy.5 = bf16[32,8,256]{2,1,0:T(8,128)(2,1)} copy(bf16[32,8,256]{2,1,0:T(8,128)(2,1)S(1)} %shard_map.37) | data formatting | bytes 262144
